TPU v7x, 256 devices: a whole 4x4x8 slice. The times are simulated.
256 devices in a mesh: kv: 32 (over z, y_lo, core), batch: 8 (over y_hi, x).
Axes of the slice: x: 4, y: 4 (y_hi: 2, y_lo: 2; y = y_hi * 2 + y_lo), z: 8, core: 2. Of those that a mesh axis runs over, the one named last changes fastest.
Arguments:
- queries: bfloat16 [256, 4, 32, 128], P(('kv', 'batch')), may hold values from -200 to 200
- prefix_keys: bfloat16 [16384, 16, 128], P(('kv', 'batch')), may hold values from -12 to 12
- prefix_values: bfloat16 [16384, 16, 128], P(('kv', 'batch')), may hold values from -12 to 12
- suffix_keys: bfloat16 [256, 1024, 16, 128], P(('kv', 'batch')), may hold values from -14 to 14
- suffix_values: bfloat16 [256, 1024, 16, 128], P(('kv', 'batch')), may hold values from -12 to 12
- lengths: int32 [256], P(('kv', 'batch')), may hold values from 256 to 1024, as said below
Outputs:
- attended: bfloat16 [256, 4, 32, 128], P(('kv', 'batch'))
Inputs may be any that keep to these rules, and one draw needn't show every extreme that they name: `lengths`: each sequence's own cache holds its 4 new tokens in its last used slots; some sequence fills all 1024 slots.
All inputs are finite; a program needn't handle non-finite values.
Results may differ from a plain program's by a relative error of at most 0.0045.
Values may be sent and summed in bfloat16 or wider, within the bound.
A program may use at most 64 MiB of HBM per device.

v0:
```python
import jax
import jax.numpy as jnp
from jax import lax
from jax.sharding import PartitionSpec as P

QUERY_SCALE = 144


masked_score = -1e30


def in_one_piece(arrays, axis, dim, along):
    ends, at = ([], 0)
    for a in arrays[:-1]:
        at += a.shape[along]
        ends.append(at)
    both = jnp.concatenate(arrays, axis=along)
    return tuple(jnp.split(lax.all_gather(both, axis, axis=dim, tiled=True), ends, axis=along))


def in_order(parts, dim):
    parts = jnp.moveaxis(parts, 0, dim)
    lengths = parts.shape
    return parts.reshape(*lengths[:dim], lengths[dim] * lengths[dim + 1], *lengths[dim + 2 :])


def from_everyone(shard, axis):
    size = lax.axis_size(axis)
    return lax.all_to_all(
        jnp.broadcast_to(shard[None], (size, *shard.shape)), axis, 0, 0, tiled=True
    )


def gathered_copies(shard, axis, dim):
    return in_order(from_everyone(shard, axis), dim)


def body(queries, prefix_keys, prefix_values, suffix_keys, suffix_values, lengths):
    scaling = QUERY_SCALE ** (-0.5)
    slab_keys, slab_values = in_one_piece((prefix_keys, prefix_values), "batch", 0, 1)
    group_rows = gathered_copies(queries, "kv", 0)
    count, new_tokens, heads, depth = group_rows.shape
    kv_heads = slab_keys.shape[1]
    queries_per_group = heads // kv_heads
    shaped = group_rows.reshape(count, new_tokens, kv_heads, queries_per_group, depth)
    scores = (
        jnp.einsum("bjgrd,pgd->bjgrp", shaped, slab_keys, preferred_element_type=jnp.float32)
        * scaling
    )
    top_prompt = jnp.max(scores, -1)
    weights = jnp.exp(scores - top_prompt[..., None])
    sum_prompt = jnp.sum(weights, -1)
    out_prompt = jnp.einsum(
        "bjgrp,pgd->bjgrd",
        weights.astype(jnp.bfloat16),
        slab_values,
        preferred_element_type=jnp.float32,
    )
    partial_value = (
        out_prompt.reshape(count, new_tokens, heads, depth),
        top_prompt.reshape(count, new_tokens, heads),
        sum_prompt.reshape(count, new_tokens, heads),
    )
    own_count = queries.shape[0]
    received = (
        lax.all_to_all(partial_value[0], "kv", split_axis=0, concat_axis=0, tiled=True),
        lax.all_to_all(partial_value[1], "kv", split_axis=0, concat_axis=0, tiled=True),
        lax.all_to_all(partial_value[2], "kv", split_axis=0, concat_axis=0, tiled=True),
    )
    sources = count // own_count
    outs_all = received[0].reshape(sources, own_count, new_tokens, heads, depth)
    tops_all = received[1].reshape(sources, own_count, new_tokens, heads)
    sums_all = received[2].reshape(sources, own_count, new_tokens, heads)
    top_p = jnp.max(tops_all, 0)
    factors = jnp.exp(tops_all - top_p[None])
    out_p = jnp.sum(outs_all * factors[..., None], 0)
    sum_p = jnp.sum(sums_all * factors, 0)
    own_shaped = queries.reshape(own_count, new_tokens, kv_heads, queries_per_group, depth)
    suffix_scores = (
        jnp.einsum("sjgrd,stgd->sjgrt", own_shaped, suffix_keys, preferred_element_type=jnp.float32)
        * scaling
    )
    slots = suffix_keys.shape[1]
    limits = lengths[:, None] - new_tokens + 1 + jnp.arange(new_tokens, dtype=jnp.int32)[None, :]
    visible = jnp.arange(slots, dtype=jnp.int32)[None, None, :] < limits[:, :, None]
    suffix_scores = jnp.where(visible[:, :, None, None, :], suffix_scores, masked_score)
    top_own = jnp.max(suffix_scores, -1)
    own_weights = jnp.exp(suffix_scores - top_own[..., None])
    sum_own = jnp.sum(own_weights, -1)
    out_own = jnp.einsum(
        "sjgrt,stgd->sjgrd",
        own_weights.astype(jnp.bfloat16),
        suffix_values,
        preferred_element_type=jnp.float32,
    )
    out_own = out_own.reshape(own_count, new_tokens, heads, depth)
    top_own = top_own.reshape(own_count, new_tokens, heads)
    sum_own = sum_own.reshape(own_count, new_tokens, heads)
    larger = jnp.maximum(top_p, top_own)
    factor_prompt = jnp.exp(top_p - larger)
    factor_own = jnp.exp(top_own - larger)
    numerator = out_p * factor_prompt[..., None] + out_own * factor_own[..., None]
    total = sum_p * factor_prompt + sum_own * factor_own
    return (numerator / total[..., None]).astype(jnp.bfloat16)


def solution(mesh):
    return jax.shard_map(
        body,
        mesh=mesh,
        in_specs=(
            P(("kv", "batch"), None, None, None),
            P(("kv", "batch"), None, None),
            P(("kv", "batch"), None, None),
            P(("kv", "batch"), None, None, None),
            P(("kv", "batch"), None, None, None),
            P(("kv", "batch")),
        ),
        out_specs=P(("kv", "batch"), None, None, None),
        check_vma=False,
    )
```

profile of v0, /device:TPU:1, one launch (start us, length us, event | category | flops | bytes accessed | tf_op | source)
XLA Modules:
  0.0 194.7 jit_solution(12833007841730563301)
XLA Ops:
  6.5 1.0 copy.72
  7.6 1.0 copy.71
  8.6 0.8 pad_maximum_fusion
  9.4 1.0 broadcast_in_dim.13
  10.4 39.0 %all_to_all.20 = bf16[32,1,4,32,128]{4,3,2,1,0:T(8,128)(2,1)S(1)} all-to-all(bf16[32,1,4,32,128]{4,3,2,1,0:T(8,128)(2,1)S(1)} %broadcast_in_dim.13), channel_id=1, replica_groups=mesh['kv'=32,'batch'=8] {'kv'}, dimensions={0} | all-to-all | bytes 2097152 | tf_op jit(solution)/shard_map/all_to_all | solution.py:29
  49.4 42.3 %all-gather.2.cloned.1.call-done = bf16[512,32,128]{2,0,1:T(8,128)(2,1)} async-done(((bf16[64,32,128]{2,0,1:T(8,128)(2,1)}), bf16[512,32,128]{2,0,1:T(8,128)(2,1)}) %all-gather.2.cloned.1.call-update) | async-done | bytes 4194320 | tf_op jit(solution)/shard_map/all_gather | solution.py:18
  91.7 3.1 %bitcast_reduce_fusion = (f32[32,4,16,2]{0,3,1,2:T(2,128)S(1)}, f32[16,512,32,4,2]{1,2,4,3,0:T(8,128)S(1)}) fusion(bf16[32,4,16,2,128]{4,3,2,1,0:T(2,128)(2,1)S(1)} %bitcast.68, bf16[512,32,128]{2,0,1:T(8,128)(2,1)} %all-gather.2.cloned.1.call-done), kind=kOutput, calls=%fused_computation.1 | convolution fusion | flops 541061120 | bytes 11550720 | tf_op jit(solution)/shard_map/bjgrd,pgd->bjgrp/dot_general | solution.py:47
  94.9 2.2 %fusion.1 = f32[32,4,16,2]{0,3,1,2:T(2,128)S(1)} fusion(f32[16,512,32,4,2]{1,2,4,3,0:T(8,128)S(1)} %get-tuple-element.11, f32[32,4,16,2]{0,3,1,2:T(2,128)S(1)} %get-tuple-element.10), kind=kLoop, calls=%fused_computation.3 | loop fusion | flops 6287360 | bytes 8421376 | tf_op jit(solution)/shard_map/reduce_sum | solution.py:52
  97.1 1.0 copy-done
  98.2 0.7 reshape.222
  98.9 8.6 %all-to-all-start.3 = ((f32[32,1,128]{2,1,0:T(1,128)}), f32[32,1,128]{2,1,0:T(1,128)S(1)}, u32[]{:S(2)}, u32[]{:S(2)}) async-start(f32[32,1,128]{2,1,0:T(1,128)} %reshape.222), calls=%async_computation.3 | async-start | bytes 32768 | tf_op jit(solution)/shard_map/all_to_all | solution.py:68
  107.6 0.7 reshape.220
  108.4 7.0 %all-to-all-done.3 = f32[32,1,128]{2,1,0:T(1,128)S(1)} async-done(((f32[32,1,128]{2,1,0:T(1,128)}), f32[32,1,128]{2,1,0:T(1,128)S(1)}, u32[]{:S(2)}, u32[]{:S(2)}) %all-to-all-start.3) | async-done | bytes 16416 | tf_op jit(solution)/shard_map/all_to_all | solution.py:68
  115.3 4.1 %all-to-all-start.2 = ((f32[32,1,128]{2,1,0:T(1,128)}), f32[32,1,128]{2,1,0:T(1,128)S(1)}, u32[]{:S(2)}, u32[]{:S(2)}) async-start(f32[32,1,128]{2,1,0:T(1,128)} %reshape.220), calls=%async_computation.2 | async-start | bytes 32768 | tf_op jit(solution)/shard_map/all_to_all | solution.py:67
  119.4 5.8 %fusion.12 = f32[32,4,16,2,128]{4,0,3,1,2:T(8,128)S(1)} fusion(f32[16,512,32,4,2]{1,2,4,3,0:T(8,128)} %copy-done, f32[32,4,16,2]{0,3,1,2:T(2,128)S(1)} %get-tuple-element.10, bf16[512,32,128]{2,0,1:T(8,128)(2,1)} %all-gather.2.cloned.1.call-done), kind=kOutput, calls=%fused_computation.16 | convolution fusion | flops 543162368 | bytes 12599296 | tf_op jit(solution)/shard_map/bjgrp,pgd->bjgrd/dot_general | solution.py:53
  125.6 2.6 %copy.76 = f32[32,4,32,128]{3,2,1,0:T(8,128)} copy(f32[32,4,32,128]{3,0,2,1:T(8,128)S(1)} %bitcast.67) | data formatting | bytes 4194304 | tf_op jit(solution)/shard_map/reshape | solution.py:60
  128.1 8.4 %all-to-all-start.1 = ((f32[32,4,32,128]{3,2,1,0:T(8,128)}), f32[32,4,32,128]{3,2,1,0:T(8,128)S(1)}, u32[]{:S(2)}, u32[]{:S(2)}) async-start(f32[32,4,32,128]{3,2,1,0:T(8,128)} %copy.76), calls=%async_computation.1 | async-start | bytes 4194304 | tf_op jit(solution)/shard_map/all_to_all | solution.py:66
  137.3 4.7 %fusion.42 = (f32[4,16,2]{2,0,1:T(4,128)S(1)}, f32[1,4,16,2,1024]{4,3,1,2,0:T(2,128)S(1)}) fusion(bf16[4,16,2,128]{3,2,1,0:T(2,128)(2,1)S(1)} %bitcast.75, bf16[1024,16,128,1]{2,1,0,3:T(8,128)(2,1)} %bitcast.76, pred[4,1024]{1,0:T(4,128)(4,1)S(1)} %iota_compare_fusion), kind=kOutput, calls=%fused_computation.43 | convolution fusion | flops 33947520 | bytes 4755968 | tf_op jit(solution)/shard_map/sjgrd,stgd->sjgrt/dot_general | solution.py:80
  142.2 4.7 %fusion.21 = f32[1,4,16,2,128]{4,3,1,2,0:T(2,128)S(1)} fusion(bf16[1024,16,128,1]{2,1,0,3:T(8,128)(2,1)} %bitcast.77, f32[1,4,16,2,1024]{4,3,1,2,0:T(2,128)S(1)} %get-tuple-element.13, f32[4,16,2]{2,0,1:T(4,128)S(1)} %get-tuple-element.12), kind=kOutput, calls=%fused_computation.19 | convolution fusion | flops 33816576 | bytes 4784640 | tf_op jit(solution)/shard_map/sjgrt,stgd->sjgrd/dot_general | solution.py:90
  148.3 0.7 reduce.8
  149.1 0.7 reduce.9
  150.0 36.4 %all-to-all-done.1 = f32[32,4,32,128]{3,2,1,0:T(8,128)S(1)} async-done(((f32[32,4,32,128]{3,2,1,0:T(8,128)}), f32[32,4,32,128]{3,2,1,0:T(8,128)S(1)}, u32[]{:S(2)}, u32[]{:S(2)}) %all-to-all-start.1) | async-done | bytes 2097184 | tf_op jit(solution)/shard_map/all_to_all | solution.py:66
  186.4 0.7 multiply_reduce_fusion
  187.1 0.7 fusion.35
  (25 shorter events, 2.6 us)
Async XLA Ops:
  6.5 85.2 %all-gather.2.cloned.1.call-start = ((), (), s32[]{:S(2)}) async-start(), calls=%async_computation.4 | async-start | bytes 4718592 | tf_op jit(solution)/shard_map/all_gather | solution.py:18
  94.9 3.2 %copy-start = (f32[16,512,32,4,2]{1,2,4,3,0:T(8,128)}, f32[16,512,32,4,2]{1,2,4,3,0:T(8,128)S(1)}, u32[]{:S(2)}) copy-start(f32[16,512,32,4,2]{1,2,4,3,0:T(8,128)S(1)} %get-tuple-element.11) | copy-start | bytes 25165828
  98.9 16.4 %all-to-all-start.3 = ((f32[32,1,128]{2,1,0:T(1,128)}), f32[32,1,128]{2,1,0:T(1,128)S(1)}, u32[]{:S(2)}, u32[]{:S(2)}) async-start(f32[32,1,128]{2,1,0:T(1,128)} %reshape.222), calls=%async_computation.3 | async-start | bytes 32768 | tf_op jit(solution)/shard_map/all_to_all | solution.py:68
  115.3 12.8 %all-to-all-start.2 = ((f32[32,1,128]{2,1,0:T(1,128)}), f32[32,1,128]{2,1,0:T(1,128)S(1)}, u32[]{:S(2)}, u32[]{:S(2)}) async-start(f32[32,1,128]{2,1,0:T(1,128)} %reshape.220), calls=%async_computation.2 | async-start | bytes 32768 | tf_op jit(solution)/shard_map/all_to_all | solution.py:67
  125.6 11.7 %copy-start.1 = (bf16[1,4,32,128]{3,2,1,0:T(8,128)(2,1)S(1)}, bf16[1,4,32,128]{3,2,1,0:T(8,128)(2,1)}, u32[]{:S(2)}) copy-start(bf16[1,4,32,128]{3,2,1,0:T(8,128)(2,1)} %param.6) | copy-start | bytes 98308
  128.1 58.3 %all-to-all-start.1 = ((f32[32,4,32,128]{3,2,1,0:T(8,128)}), f32[32,4,32,128]{3,2,1,0:T(8,128)S(1)}, u32[]{:S(2)}, u32[]{:S(2)}) async-start(f32[32,4,32,128]{3,2,1,0:T(8,128)} %copy.76), calls=%async_computation.1 | async-start | bytes 4194304 | tf_op jit(solution)/shard_map/all_to_all | solution.py:66
Sparse Core Ops, SparseCore 0:
  10.0 81.7 all-gather.1
where the time goes:
time: 195 us
  waiting for transfers between devices  85.7 us (44%)
  blocking collectives  39 us (20%)
  starting transfers between devices  21 us (11%)
  matrix products  18.3 us (9%)
  between operations  14.2 us (7%)
  local copies, waits for them, and re-layouts  9.84 us (5%)
  other arithmetic  6.58 us (3%)
    all_gather x1, waiting for transfers between devices, in_one_piece(): lax.all_gather(both, axis, axis=dim, tiled=True)  42.3 us
    all_to_all x1, blocking collectives, from_everyone(): lax.all_to_all(jnp.broadcast_to(shard[None], (size, *shard.shape)), axis,...  39 us
    all_to_all x1, waiting for transfers between devices, body(): lax.all_to_all(partial_value[0], 'kv', split_axis=0, concat_axis=0, tiled...  36.4 us
    all_to_all x1, starting transfers between devices, body(): lax.all_to_all(partial_value[2], 'kv', split_axis=0, concat_axis=0, tiled...  8.58 us
    all_to_all x1, starting transfers between devices, body(): lax.all_to_all(partial_value[0], 'kv', split_axis=0, concat_axis=0, tiled...  8.38 us
    all_to_all x1, waiting for transfers between devices, body(): lax.all_to_all(partial_value[2], 'kv', split_axis=0, concat_axis=0, tiled...  6.97 us
    dot_general x1, matrix products, body(): jnp.einsum('bjgrp,pgd->bjgrd', weights.astype(jnp.bfloat16), slab_values,...  5.84 us
    dot_general x1, matrix products, body(): jnp.einsum('sjgrd,stgd->sjgrt', own_shaped, suffix_keys, preferred_elemen...  4.68 us
  transfers between devices with their start and end apart: 4, of which 3 were waited for; matrix products, arithmetic and copies ran while one was open for 12% of the time, Pallas kernels for 0%

commit v1 on v0

v1 whole, which is shorter than its diff:
```python
import functools
import math

import jax
import jax.numpy as jnp
from jax import lax
from jax.experimental import pallas as pl
from jax.experimental.pallas import tpu as pltpu
from jax.sharding import PartitionSpec as P

QUERY_SCALE = 144
LOG2_SCALE = QUERY_SCALE ** (-0.5) * math.log2(math.e)
HIDDEN = -1e30

HEADS = 8
CHUNKS = 4
PER = HEADS // CHUNKS
TALL = 144
PIECE = 2048

f32, bf16 = jnp.float32, jnp.bfloat16
MESH = pl.DeviceIdType.MESH
ROWS_BY_ROWS = (((1,), (1,)), ((), ()))


def place():
    kv, b = lax.axis_index("kv"), lax.axis_index("batch")
    return b % 4, (b // 4) * 2 + (kv // 2) % 2, kv // 4, kv % 2


def device(dx=0, dy=0, dz=0, e=0):
    x, y, z, c = place()
    x, y, z = (x + dx) % 4, (y + dy) % 4, (z + dz) % 8
    c = (c + e) % 2
    return (z * 2 + y % 2) * 2 + c, (y // 2) * 4 + x


def iota(shape, dim):
    return lax.broadcasted_iota(jnp.int32, shape, dim)


def one_hot(shape, wanted):
    return jnp.where(iota(shape, 1) == wanted(iota(shape, 0)), 1.0, 0.0).astype(bf16)


def dot(a, b):
    return jnp.dot(a, b, preferred_element_type=f32)


def dot_t(a, b):
    return lax.dot_general(a, b, ROWS_BY_ROWS, preferred_element_type=f32)


def in_two(v):
    high = v.astype(bf16).astype(f32)
    return high, (v - high).astype(bf16).astype(f32)


def packed_stats(mh, ml, total):
    lh, ll = in_two(total)
    row = iota((16, mh.shape[1]), 0)
    out = jnp.where(row == 0, mh, jnp.where(row == 1, ml, jnp.where(row == 2, lh, ll)))
    return jnp.where(row < 4, out, 0.0).astype(bf16)


def stats_of(block):
    st = block[128:TALL, :].astype(f32)
    return st[0:1] + st[1:2], st[2:3] + st[3:4]


def merged(blocks):
    stats = [stats_of(b) for b in blocks]
    top = functools.reduce(jnp.maximum, [m for m, _ in stats])
    out, total = 0.0, 0.0
    for b, (m, l) in zip(blocks, stats):
        w = jnp.exp2(m - top)
        out = out + b[0:128, :].astype(f32) * w
        total = total + l * w
    return out, top, total


def kernel(
    len_ref, q_hbm, k_hbm, v_hbm, sk_hbm, sv_hbm, out_ref,
    qin, kvin, sk, sv, kv, kvs, qy, qs, qsuf, xs, r1, x2, perm, ys, r2,
    so, sm, sl, suf, sufr, fin, finr, local_sem, send_sem, recv_sem,
):
    x, y, z, c = place()
    peers = [dict(dx=d, e=e) for d in (1, 3) for e in (0, 1)] + [dict(e=1)]
    peers += [dict(dy=d) for d in (1, 2, 3)] + [dict(dz=d, e=e) for d in range(1, 8) for e in (0, 1)]
    barrier = pltpu.get_barrier_semaphore()
    for p in peers:
        pl.semaphore_signal(barrier, inc=1, device_id=device(**p), device_id_type=MESH)

    loads = [
        pltpu.make_async_copy(src, dst, local_sem.at[i])
        for i, (src, dst) in enumerate(
            [(q_hbm, qin), (k_hbm, kvin.at[0]), (v_hbm, kvin.at[1]), (sk_hbm, sk), (sv_hbm, sv)]
        )
    ]
    for load in loads:
        load.start()

    started = []

    def send(src, dst, **to):
        i = len(started)
        copy = pltpu.make_async_remote_copy(
            src_ref=src, dst_ref=dst, send_sem=send_sem.at[i], recv_sem=recv_sem.at[i],
            device_id=device(**to), device_id_type=MESH,
        )
        copy.start()
        started.append(copy)
        return copy

    loads[0].wait()

    def query_row(row, e, g):
        j, r = (row % 8) // 2, row % 2
        return j * 32 + ((e + c) % 2 * 8 + g) * 2 + r

    q = qin[...]
    moved = dot(one_hot((128, 128), lambda o: query_row(o, o // 64, (o // 8) % 8)), q)
    qy[0, 0, 0] = moved[:64].astype(bf16).reshape(HEADS, 8, 128)
    qs[...] = moved[64:].astype(bf16).reshape(HEADS, 8, 128)
    qsuf[...] = dot(one_hot((128, 128), lambda o: query_row(o, (o // 8) % 2, o // 16)), q).astype(bf16)

    def head_row(o):
        big = o // 16
        return (o % 16) * 16 + (big // 8 + c) % 2 * 8 + big % 8

    move = one_hot((256, 256), head_row)
    loads[1].wait()
    loads[2].wait()
    for t in range(2):
        for b in range(4):
            m = dot(move, kvin[t, 256 * b : 256 * b + 256, :]).astype(bf16).reshape(16, 16, 128)
            kv[t, :, 0, 16 * b : 16 * b + 16, :] = m[:8]
            kvs[t, :, 16 * b : 16 * b + 16, :] = m[8:]

    pl.semaphore_wait(barrier, len(peers))

    def heads_of(k):
        return pl.ds(k * PER, PER)

    kv_copies = [dict() for _ in range(CHUNKS)]

    def send_kv(k):
        h = heads_of(k)
        for dx, e in ((1, 0), (3, 1), (1, 1), (3, 0), (0, 1)):
            src = kvs.at[:, h] if e else kv.at[:, h, 0]
            kv_copies[k][dx, e] = send(src, kv.at[:, h, 2 * dx + e], dx=dx, e=e)

    def forward_kv(k):
        h = heads_of(k)
        kv_copies[k][1, 0].wait_recv()
        kv_copies[k][2, 0] = send(kv.at[:, h, 2], kv.at[:, h, 4], dx=1)
        kv_copies[k][3, 1].wait_recv()
        kv_copies[k][2, 1] = send(kv.at[:, h, 7], kv.at[:, h, 5], dx=3)

    send_kv(0)
    q1 = []
    for dz in (4, 3, 5, 2, 6, 1, 7, 0):
        for e in (0, 1):
            if dz or e:
                q1.append(send(qs if e else qy.at[0, 0, 0], qy.at[0, dz, e], dz=dz, e=e))
    send_kv(1)

    so[...] = jnp.zeros_like(so)
    sl[...] = jnp.zeros_like(sl)
    sm[...] = jnp.full_like(sm, HIDDEN)
    loads[3].wait()
    loads[4].wait()
    length = len_ref[0]

    def suffix_piece(i, _):
        row, lane = iota((128, 128), 0), iota((128, 128), 1)
        head = ((row // 8) % 2 + c) % 2 * 8 + row // 16
        bias = jnp.where(lane % 16 == head, 0.0, HIDDEN)
        room = length - 3 + (row % 8) // 2 - lane // 16
        at = pl.ds(pl.multiple_of(i * PIECE, PIECE), PIECE)
        raw = dot_t(qsuf[...], sk[at, :])
        parts = []
        for t in range(PIECE // 128):
            part = raw[:, 128 * t : 128 * t + 128] * LOG2_SCALE + bias
            parts.append(jnp.where(room > i * (PIECE // 16) + 8 * t, part, HIDDEN))
        old = sm[...]
        top = jnp.maximum(old, jnp.max(functools.reduce(jnp.maximum, parts), 1, keepdims=True))
        weights = [jnp.exp2(part - top) for part in parts]
        shrink = jnp.exp2(old - top)
        sm[...] = top
        sl[...] = sl[...] * shrink + jnp.sum(functools.reduce(jnp.add, weights), 1, keepdims=True)
        rounded = jnp.concatenate([w.astype(bf16) for w in weights], axis=1)
        so[...] = so[...] * shrink + dot(rounded, sv[at, :])
        return 0

    lax.fori_loop(0, 3, suffix_piece, 0)
    forward_kv(0)
    send_kv(2)
    lax.fori_loop(3, 6, suffix_piece, 0)
    for copy in q1:
        copy.wait_recv()
    q2 = []

    def send_q(k):
        h = heads_of(k)
        q2.append([send(qy.at[0, :, :, h], qy.at[dy, :, :, h], dy=dy) for dy in (2, 1, 3)])

    for k in range(CHUNKS):
        send_q(k)
    forward_kv(1)
    send_kv(3)
    lax.fori_loop(6, 16384 // PIECE, suffix_piece, 0)

    eye = one_hot((128, 128), lambda o: o)
    mh, ml = in_two(sm[...])
    adjust = jnp.exp2(sm[...] - (mh + ml))
    lh, ll = in_two(sl[...] * adjust)
    suf[0:128, :] = dot_t(eye, (so[...] * adjust).astype(bf16)).astype(bf16)
    col = iota((128, 128), 1)
    columns = jnp.where(col == 0, mh, jnp.where(col == 1, ml, jnp.where(col == 2, lh, ll)))
    columns = jnp.where(col < 4, columns, 0.0).astype(bf16)
    suf[128:TALL, :] = dot_t(one_hot((16, 128), lambda o: o), columns).astype(bf16)
    suffix_copy = send(suf, sufr, e=1)
    for g in range(HEADS):
        perm[128 * g : 128 * g + 128, :] = one_hot(
            (128, 1024), lambda o, g=g: (o // 16) * 128 + g * 16 + o % 16
        )
    forward_kv(2)

    def prompt_head(g, _):
        keys = kv[0, g].reshape(512, 128)
        values = kv[1, g].reshape(512, 128)
        rows = qy[:, :, :, g].astype(f32).reshape(512, 128).astype(bf16)
        scores = dot_t(keys, rows) * LOG2_SCALE
        mh, ml = in_two(jnp.max(scores, 0, keepdims=True))
        weights = jnp.exp2(scores - (mh + ml))
        stats = packed_stats(mh, ml, jnp.sum(weights, 0, keepdims=True))
        out = dot(dot_t(eye, values).astype(bf16), weights.astype(bf16)).astype(bf16)
        for dy in range(4):
            xs[dy, g, 0:128, :] = out[:, 128 * dy : 128 * dy + 128]
            xs[dy, g, 128:TALL, :] = stats[:, 128 * dy : 128 * dy + 128]
        return 0

    rs1 = []
    for k in range(CHUNKS):
        for copy in q2[k]:
            copy.wait_recv()
        for at in ((0, 1), (1, 1), (3, 0), (2, 0), (2, 1)):
            kv_copies[k][at].wait_recv()
        lax.fori_loop(k * PER, (k + 1) * PER, prompt_head, 0)
        h = heads_of(k)
        rs1.append([send(xs.at[dy, h], r1.at[dy, h], dy=4 - dy) for dy in (2, 1, 3)])
        if k == 0:
            forward_kv(3)

    for k in range(CHUNKS):
        for copy in rs1[k]:
            copy.wait_recv()
        for g in range(k * PER, (k + 1) * PER):
            out, top, total = merged([xs[0, g]] + [r1[dy, g] for dy in range(1, 4)])
            mh, ml = in_two(top)
            adjust = jnp.exp2(top - (mh + ml))
            x2[0:128, 128 * g : 128 * g + 128] = (out * adjust).astype(bf16)
            x2[128:TALL, 128 * g : 128 * g + 128] = packed_stats(mh, ml, total * adjust)

    moved = dot(x2[...], perm[...]).astype(bf16)
    for dz in range(8):
        ys[dz] = moved[:, 128 * dz : 128 * dz + 128]
    rs2 = [send(ys.at[dz], r2.at[dz], dz=8 - dz) for dz in (4, 3, 5, 2, 6, 1, 7)]

    suffix_copy.wait_recv()
    lane = iota((TALL, 128), 1)
    own = jnp.where((lane // 8) % 2 == 0, suf[...].astype(f32), sufr[...].astype(f32))
    for copy in rs2:
        copy.wait_recv()
    out, _, total = merged([own, ys[0]] + [r2[dz] for dz in range(1, 8)])
    attended = (out / total).astype(bf16)

    def final_lane(o):
        e, j, g, r = o // 64, (o // 16) % 4, (o // 2) % 8, o % 2
        return g * 16 + e * 8 + j * 2 + r

    rows = dot_t(one_hot((128, 128), final_lane), attended).astype(bf16)
    fin[...] = rows[64:].reshape(4, 16, 128)
    last = send(fin, finr, e=1)
    out_ref[:, pl.ds(c, 1)] = rows[:64].reshape(4, 1, 16, 128)
    last.wait_recv()
    out_ref[:, pl.ds(1 - c, 1)] = finr[...].reshape(4, 1, 16, 128)
    for copy in started:
        copy.wait_send()


COPIES = 15 + 7 * CHUNKS + 3 * CHUNKS * 2 + 7 + 2


def body(queries, prefix_keys, prefix_values, suffix_keys, suffix_values, lengths):
    vmem, anyspace = pltpu.VMEM, pl.BlockSpec(memory_space=pl.ANY)
    out = pl.pallas_call(
        kernel,
        name="attend",
        out_shape=jax.ShapeDtypeStruct((4, 2, 16, 128), bf16),
        in_specs=[pl.BlockSpec(memory_space=pltpu.SMEM)] + [anyspace] * 5,
        out_specs=pl.BlockSpec(memory_space=vmem),
        scratch_shapes=[
            vmem((128, 128), bf16),
            vmem((2, 1024, 128), bf16),
            vmem((16384, 128), bf16),
            vmem((16384, 128), bf16),
            vmem((2, HEADS, 8, 64, 128), bf16),
            vmem((2, HEADS, 64, 128), bf16),
            vmem((4, 8, 2, HEADS, 8, 128), bf16),
            vmem((HEADS, 8, 128), bf16),
            vmem((128, 128), bf16),
            vmem((4, HEADS, TALL, 128), bf16),
            vmem((4, HEADS, TALL, 128), bf16),
            vmem((TALL, 1024), bf16),
            vmem((1024, 1024), bf16),
            vmem((8, TALL, 128), bf16),
            vmem((8, TALL, 128), bf16),
            vmem((128, 128), f32),
            vmem((128, 128), f32),
            vmem((128, 128), f32),
            vmem((TALL, 128), bf16),
            vmem((TALL, 128), bf16),
            vmem((4, 16, 128), bf16),
            vmem((4, 16, 128), bf16),
            pltpu.SemaphoreType.DMA((5,)),
            pltpu.SemaphoreType.DMA((COPIES,)),
            pltpu.SemaphoreType.DMA((COPIES,)),
        ],
        compiler_params=pltpu.CompilerParams(
            collective_id=0, has_side_effects=True, vmem_limit_bytes=48 * 2**20
        ),
    )(
        lengths,
        queries.reshape(128, 128),
        prefix_keys.reshape(1024, 128),
        prefix_values.reshape(1024, 128),
        suffix_keys.reshape(16384, 128),
        suffix_values.reshape(16384, 128),
    )
    return out.reshape(1, 4, 32, 128)


def solution(mesh):
    return jax.shard_map(
        body,
        mesh=mesh,
        in_specs=(
            P(("kv", "batch"), None, None, None),
            P(("kv", "batch"), None, None),
            P(("kv", "batch"), None, None),
            P(("kv", "batch"), None, None, None),
            P(("kv", "batch"), None, None, None),
            P(("kv", "batch")),
        ),
        out_specs=P(("kv", "batch"), None, None, None),
        check_vma=False,
    )
```

time: 195 us -> 62.4 us (0.32)
  waiting for transfers between devices: 85.7 us -> 0 us
  Pallas kernels: 0 us -> 56 us
  blocking collectives: 39 us -> 0 us
  starting transfers between devices: 21 us -> 0 us
  matrix products: 18.3 us -> 0 us
  between operations: 14.2 us -> 0.67 us
  other arithmetic: 6.58 us -> 0 us
  local copies, waits for them, and re-layouts: 9.84 us -> 5.45 us
    pallas_call x0 -> x1, Pallas kernels: none -> 56 us  [body(): pl.pallas_call(kernel, name='attend', out_shape=jax.ShapeDtypeStruct((4,...]
    all_to_all x3 -> x0, waiting for transfers between devices: 43.4 us -> none  [the longest x1 36.4 us: body(): lax.all_to_all(partial_value[0], 'kv', split_axis=0, concat_axis=0, tiled...]
    all_gather x1 -> x0, waiting for transfers between devices: 42.3 us -> none  [in_one_piece(): lax.all_gather(both, axis, axis=dim, tiled=True)]
    all_to_all x1 -> x0, blocking collectives: 39 us -> none  [from_everyone(): lax.all_to_all(jnp.broadcast_to(shard[None], (size, *shard.shape)), axis,...]
    all_to_all x3 -> x0, starting transfers between devices: 21 us -> none  [the longest x1 8.58 us: body(): lax.all_to_all(partial_value[2], 'kv', split_axis=0, concat_axis=0, tiled...]
    dot_general x4 -> x0, matrix products: 18.3 us -> none  [the longest x1 5.84 us: body(): jnp.einsum('bjgrp,pgd->bjgrd', weights.astype(jnp.bfloat16), slab_values,...]
    reduce_sum x4 -> x0, other arithmetic: 3.5 us -> none  [the longest x1 2.21 us: body(): sum_prompt = jnp.sum(weights, -1)]
    reshape x5 -> x0, local copies, waits for them, and re-layouts: 2.9 us -> none  [the longest x1 2.57 us: body(): out_prompt.reshape(count, new_tokens, heads, depth)]
  transfers between devices with their start and end apart: 4 -> 0, of which waited for: 3 -> 0; matrix products, arithmetic and copies ran while one was open for 12% -> 0% of each run, Pallas kernels for 0% -> 0%
where the time goes in v1:
time: 62.4 us; the launch traced here: 62.1 us
  Pallas kernels  56 us (90%)
  local copies, waits for them, and re-layouts  5.45 us (9%)
  between operations  0.67 us (1%)
    pallas_call x1, Pallas kernels, body(): pl.pallas_call(kernel, name='attend', out_shape=jax.ShapeDtypeStruct((4,...  56 us
    unnamed x9, local copies, waits for them, and re-layouts  5.45 us

profile of v1, /device:TPU:1, one launch (start us, length us, event | category | flops | bytes accessed | tf_op | source)
XLA Modules:
  0.0 62.1 jit_solution(11651126042900505337)
XLA Ops:
  0.7 0.0 copy-start
  0.7 2.2 %copy-done = bf16[1,1024,16,128]{3,2,1,0:T(8,128)(2,1)S(1)} copy-done((bf16[1,1024,16,128]{3,2,1,0:T(8,128)(2,1)S(1)}, bf16[1,1024,16,128]{3,2,1,0:T(8,128)(2,1)}, u32[]{:S(2)}) %copy-start) | copy-done | bytes 4194328
  2.8 0.0 copy-start.1
  2.8 0.9 %copy-done.1 = bf16[64,16,128]{2,1,0:T(8,128)(2,1)S(1)} copy-done((bf16[64,16,128]{2,1,0:T(8,128)(2,1)S(1)}, bf16[64,16,128]{2,1,0:T(8,128)(2,1)}, u32[]{:S(2)}) %copy-start.1) | copy-done | bytes 262168
  3.8 0.0 copy-start.2
  3.8 0.9 %copy-done.2 = bf16[64,16,128]{2,1,0:T(8,128)(2,1)S(1)} copy-done((bf16[64,16,128]{2,1,0:T(8,128)(2,1)S(1)}, bf16[64,16,128]{2,1,0:T(8,128)(2,1)}, u32[]{:S(2)}) %copy-start.2) | copy-done | bytes 262168
  4.7 0.0 copy-start.3
  4.7 0.8 %copy-done.3 = bf16[1,4,32,128]{3,2,1,0:T(8,128)(2,1)S(1)} copy-done((bf16[1,4,32,128]{3,2,1,0:T(8,128)(2,1)S(1)}, bf16[1,4,32,128]{3,2,1,0:T(8,128)(2,1)}, u32[]{:S(2)}) %copy-start.3) | copy-done | bytes 32792
  5.5 56.0 %attend.1 = bf16[4,2,16,128]{3,2,1,0:T(8,128)(2,1)S(1)} custom-call(s32[1]{0:T(128)S(6)} %copy.8.len_ref, bf16[128,128]{1,0:T(8,128)(2,1)S(1)} %bitcast.10, bf16[1024,128]{1,0:T(8,128)(2,1)S(1)} %bitcast.7, bf16[1024,128]{1,0:T(8,128)(2,1)S(1)} %bitcast.8, bf16[16384,128]{1,0:T(8,128)(2,1)S(1)} %bitcast.6, bf16[16384,128]{1,0:T(8,128)(2,1)} %bitcast.11), custom_call_target="tpu_custom_call" | custom-call | tf_op jit(solution)/shard_map/attend/pallas_call | solution.py:298
  61.5 0.6 copy.9
Async XLA Ops:
  0.7 2.2 %copy-start = (bf16[1,1024,16,128]{3,2,1,0:T(8,128)(2,1)S(1)}, bf16[1,1024,16,128]{3,2,1,0:T(8,128)(2,1)}, u32[]{:S(2)}) copy-start(bf16[1,1024,16,128]{3,2,1,0:T(8,128)(2,1)} %param.9) | copy-start | bytes 12582916
  2.8 0.9 %copy-start.1 = (bf16[64,16,128]{2,1,0:T(8,128)(2,1)S(1)}, bf16[64,16,128]{2,1,0:T(8,128)(2,1)}, u32[]{:S(2)}) copy-start(bf16[64,16,128]{2,1,0:T(8,128)(2,1)} %param.7) | copy-start | bytes 786436
  3.8 0.9 %copy-start.2 = (bf16[64,16,128]{2,1,0:T(8,128)(2,1)S(1)}, bf16[64,16,128]{2,1,0:T(8,128)(2,1)}, u32[]{:S(2)}) copy-start(bf16[64,16,128]{2,1,0:T(8,128)(2,1)} %param.8) | copy-start | bytes 786436
  4.7 0.8 %copy-start.3 = (bf16[1,4,32,128]{3,2,1,0:T(8,128)(2,1)S(1)}, bf16[1,4,32,128]{3,2,1,0:T(8,128)(2,1)}, u32[]{:S(2)}) copy-start(bf16[1,4,32,128]{3,2,1,0:T(8,128)(2,1)} %param.6) | copy-start | bytes 98308

commit v2 on v1

--- a/solution.py
+++ b/solution.py
@@ -81,12 +81,13 @@
 
 def kernel(
     len_ref, q_hbm, k_hbm, v_hbm, sk_hbm, sv_hbm, out_ref,
-    qin, kvin, sk, sv, kv, kvs, qy, qs, qsuf, xs, r1, x2, perm, ys, r2,
-    so, sm, sl, suf, sufr, fin, finr, local_sem, send_sem, recv_sem,
+    qin, kvin, sk, sv, kv, kvs, qy, qs, qsuf, xs, r1, sx, ys, r2,
+    so, sm, sl, local_sem, send_sem, recv_sem,
 ):
     x, y, z, c = place()
     peers = [dict(dx=d, e=e) for d in (1, 3) for e in (0, 1)] + [dict(e=1)]
-    peers += [dict(dy=d) for d in (1, 2, 3)] + [dict(dz=d, e=e) for d in range(1, 8) for e in (0, 1)]
+    peers += [dict(dy=d, e=e) for d in (1, 2, 3) for e in (0, 1)]
+    peers += [dict(dz=d, e=e) for d in range(1, 8) for e in (0, 1)]
     barrier = pltpu.get_barrier_semaphore()
     for p in peers:
         pl.semaphore_signal(barrier, inc=1, device_id=device(**p), device_id_type=MESH)
@@ -94,7 +95,7 @@
     loads = [
         pltpu.make_async_copy(src, dst, local_sem.at[i])
         for i, (src, dst) in enumerate(
-            [(q_hbm, qin), (k_hbm, kvin.at[0]), (v_hbm, kvin.at[1]), (sk_hbm, sk), (sv_hbm, sv)]
+            [(k_hbm, kvin.at[0]), (v_hbm, kvin.at[1]), (q_hbm, qin), (sk_hbm, sk), (sv_hbm, sv)]
         )
     ]
     for load in loads:
@@ -112,35 +113,33 @@
         started.append(copy)
         return copy
 
-    loads[0].wait()
-
-    def query_row(row, e, g):
-        j, r = (row % 8) // 2, row % 2
-        return j * 32 + ((e + c) % 2 * 8 + g) * 2 + r
-
-    q = qin[...]
-    moved = dot(one_hot((128, 128), lambda o: query_row(o, o // 64, (o // 8) % 8)), q)
-    qy[0, 0, 0] = moved[:64].astype(bf16).reshape(HEADS, 8, 128)
-    qs[...] = moved[64:].astype(bf16).reshape(HEADS, 8, 128)
-    qsuf[...] = dot(one_hot((128, 128), lambda o: query_row(o, (o // 8) % 2, o // 16)), q).astype(bf16)
+    def heads_of(k, n=1):
+        return pl.ds(k * PER, n * PER)
 
     def head_row(o):
         big = o // 16
         return (o % 16) * 16 + (big // 8 + c) % 2 * 8 + big % 8
 
     move = one_hot((256, 256), head_row)
-    loads[1].wait()
-    loads[2].wait()
     for t in range(2):
+        loads[t].wait()
         for b in range(4):
             m = dot(move, kvin[t, 256 * b : 256 * b + 256, :]).astype(bf16).reshape(16, 16, 128)
             kv[t, :, 0, 16 * b : 16 * b + 16, :] = m[:8]
             kvs[t, :, 16 * b : 16 * b + 16, :] = m[8:]
 
+    loads[2].wait()
+
+    def query_row(o):
+        e, g, j, r = o // 64, (o // 8) % 8, (o % 8) // 2, o % 2
+        return j * 32 + ((e + c) % 2 * 8 + g) * 2 + r
+
+    q = dot(one_hot((128, 128), query_row), qin[...]).astype(bf16)
+    qsuf[...] = q
+    qy[0, 0, 0] = q[:64].reshape(HEADS, 8, 128)
+    qs[...] = q[64:].reshape(HEADS, 8, 128)
+
     pl.semaphore_wait(barrier, len(peers))
-
-    def heads_of(k):
-        return pl.ds(k * PER, PER)
 
     kv_copies = [dict() for _ in range(CHUNKS)]
 
@@ -157,24 +156,34 @@
         kv_copies[k][3, 1].wait_recv()
         kv_copies[k][2, 1] = send(kv.at[:, h, 7], kv.at[:, h, 5], dx=3)
 
+    half = CHUNKS // 2
+    zy, yz = heads_of(0, half), heads_of(half, half)
+
+    def source(e, h):
+        return qs.at[h] if e else qy.at[0, 0, 0, h]
+
     send_kv(0)
-    q1 = []
-    for dz in (4, 3, 5, 2, 6, 1, 7, 0):
-        for e in (0, 1):
-            if dz or e:
-                q1.append(send(qs if e else qy.at[0, 0, 0], qy.at[0, dz, e], dz=dz, e=e))
+    q1 = [
+        send(source(e, zy), qy.at[0, dz, e, zy], dz=dz, e=e)
+        for dz in (4, 3, 5, 2, 6, 1, 7, 0) for e in (0, 1) if dz or e
+    ]
+    p1 = [
+        send(source(e, yz), qy.at[dy, 0, e, yz], dy=dy, e=e)
+        for dy in (2, 1, 3, 0) for e in (0, 1) if dy or e
+    ]
     send_kv(1)
 
     so[...] = jnp.zeros_like(so)
     sl[...] = jnp.zeros_like(sl)
     sm[...] = jnp.full_like(sm, HIDDEN)
+    sx[...] = jnp.zeros_like(sx)
     loads[3].wait()
     loads[4].wait()
     length = len_ref[0]
 
     def suffix_piece(i, _):
         row, lane = iota((128, 128), 0), iota((128, 128), 1)
-        head = ((row // 8) % 2 + c) % 2 * 8 + row // 16
+        head = (row // 64 + c) % 2 * 8 + (row // 8) % 8
         bias = jnp.where(lane % 16 == head, 0.0, HIDDEN)
         room = length - 3 + (row % 8) // 2 - lane // 16
         at = pl.ds(pl.multiple_of(i * PIECE, PIECE), PIECE)
@@ -193,39 +202,39 @@
         so[...] = so[...] * shrink + dot(rounded, sv[at, :])
         return 0
 
-    lax.fori_loop(0, 3, suffix_piece, 0)
+    def suffix(first, last):
+        lax.fori_loop(first, last, suffix_piece, 0)
+
+    suffix(0, 2)
+    for copy in p1:
+        copy.wait_recv()
+    q2 = [[] for _ in range(CHUNKS)]
+
+    def send_q_z(k):
+        h = heads_of(k)
+        q2[k] = [send(qy.at[:, 0, :, h], qy.at[:, dz, :, h], dz=dz) for dz in (4, 3, 5, 2, 6, 1, 7)]
+
+    def send_q_y(k):
+        h = heads_of(k)
+        q2[k] = [send(qy.at[0, :, :, h], qy.at[dy, :, :, h], dy=dy) for dy in (2, 1, 3)]
+
+    for k in range(half, CHUNKS):
+        send_q_z(k)
+    suffix(2, 3)
     forward_kv(0)
     send_kv(2)
-    lax.fori_loop(3, 6, suffix_piece, 0)
+    suffix(3, 5)
     for copy in q1:
         copy.wait_recv()
-    q2 = []
-
-    def send_q(k):
-        h = heads_of(k)
-        q2.append([send(qy.at[0, :, :, h], qy.at[dy, :, :, h], dy=dy) for dy in (2, 1, 3)])
-
-    for k in range(CHUNKS):
-        send_q(k)
+    for k in range(half):
+        send_q_y(k)
+    suffix(5, 6)
     forward_kv(1)
     send_kv(3)
-    lax.fori_loop(6, 16384 // PIECE, suffix_piece, 0)
+    suffix(6, 16384 // PIECE)
+    forward_kv(2)
 
     eye = one_hot((128, 128), lambda o: o)
-    mh, ml = in_two(sm[...])
-    adjust = jnp.exp2(sm[...] - (mh + ml))
-    lh, ll = in_two(sl[...] * adjust)
-    suf[0:128, :] = dot_t(eye, (so[...] * adjust).astype(bf16)).astype(bf16)
-    col = iota((128, 128), 1)
-    columns = jnp.where(col == 0, mh, jnp.where(col == 1, ml, jnp.where(col == 2, lh, ll)))
-    columns = jnp.where(col < 4, columns, 0.0).astype(bf16)
-    suf[128:TALL, :] = dot_t(one_hot((16, 128), lambda o: o), columns).astype(bf16)
-    suffix_copy = send(suf, sufr, e=1)
-    for g in range(HEADS):
-        perm[128 * g : 128 * g + 128, :] = one_hot(
-            (128, 1024), lambda o, g=g: (o // 16) * 128 + g * 16 + o % 16
-        )
-    forward_kv(2)
 
     def prompt_head(g, _):
         keys = kv[0, g].reshape(512, 128)
@@ -242,6 +251,26 @@
         return 0
 
     rs1 = []
+    rs2 = []
+
+    def over_y(k):
+        for copy in rs1[k]:
+            copy.wait_recv()
+        for i in range(PER):
+            g = k * PER + i
+            out, top, total = merged([xs[0, g]] + [r1[dy, g] for dy in range(1, 4)])
+            mh, ml = in_two(top)
+            adjust = jnp.exp2(top - (mh + ml))
+            ys[k, :, i] = dot_t(eye, (out * adjust).astype(bf16)).astype(bf16).reshape(16, 8, 128)
+            sx[k, 16 * i : 16 * i + 16, :] = packed_stats(mh, ml, total * adjust)
+        ys[k, :, PER] = dot_t(eye, sx[k]).astype(bf16).reshape(16, 8, 128)
+        rs2.append(
+            [
+                send(ys.at[k, 2 * dz + e], r2.at[k, 2 * dz + e], dz=8 - dz, e=e)
+                for dz in (4, 3, 5, 2, 6, 1, 7, 0) for e in (0, 1) if dz or e
+            ]
+        )
+
     for k in range(CHUNKS):
         for copy in q2[k]:
             copy.wait_recv()
@@ -252,45 +281,47 @@
         rs1.append([send(xs.at[dy, h], r1.at[dy, h], dy=4 - dy) for dy in (2, 1, 3)])
         if k == 0:
             forward_kv(3)
-
+        if k >= 2:
+            over_y(k - 2)
+    for k in range(CHUNKS - 2, CHUNKS):
+        over_y(k)
+
+    done = []
     for k in range(CHUNKS):
-        for copy in rs1[k]:
+        for copy in rs2[k]:
             copy.wait_recv()
-        for g in range(k * PER, (k + 1) * PER):
-            out, top, total = merged([xs[0, g]] + [r1[dy, g] for dy in range(1, 4)])
-            mh, ml = in_two(top)
-            adjust = jnp.exp2(top - (mh + ml))
-            x2[0:128, 128 * g : 128 * g + 128] = (out * adjust).astype(bf16)
-            x2[128:TALL, 128 * g : 128 * g + 128] = packed_stats(mh, ml, total * adjust)
-
-    moved = dot(x2[...], perm[...]).astype(bf16)
-    for dz in range(8):
-        ys[dz] = moved[:, 128 * dz : 128 * dz + 128]
-    rs2 = [send(ys.at[dz], r2.at[dz], dz=8 - dz) for dz in (4, 3, 5, 2, 6, 1, 7)]
-
-    suffix_copy.wait_recv()
-    lane = iota((TALL, 128), 1)
-    own = jnp.where((lane // 8) % 2 == 0, suf[...].astype(f32), sufr[...].astype(f32))
-    for copy in rs2:
-        copy.wait_recv()
-    out, _, total = merged([own, ys[0]] + [r2[dz] for dz in range(1, 8)])
-    attended = (out / total).astype(bf16)
-
-    def final_lane(o):
-        e, j, g, r = o // 64, (o // 16) % 4, (o // 2) % 8, o % 2
-        return g * 16 + e * 8 + j * 2 + r
-
-    rows = dot_t(one_hot((128, 128), final_lane), attended).astype(bf16)
-    fin[...] = rows[64:].reshape(4, 16, 128)
-    last = send(fin, finr, e=1)
-    out_ref[:, pl.ds(c, 1)] = rows[:64].reshape(4, 1, 16, 128)
-    last.wait_recv()
-    out_ref[:, pl.ds(1 - c, 1)] = finr[...].reshape(4, 1, 16, 128)
+        for e in (0, 1):
+            blocks = [ys.at[k, 0] if not (dz or e) else r2.at[k, 2 * dz + e] for dz in range(8)]
+            lane = iota((8, 128), 1)
+            mine = [(e * 8 + k * PER + i) * 8 for i in range(PER)]
+            top_own = total_own = jnp.zeros((8, 128), f32)
+            for i, at in enumerate(mine):
+                top_own = jnp.where(lane // 16 == i, sm[at : at + 8, :], top_own)
+                total_own = jnp.where(lane // 16 == i, sl[at : at + 8, :], total_own)
+            tiles = [b[PER].astype(f32) for b in blocks]
+            tops = [t + pltpu.roll(t, 127, 1) for t in tiles] + [top_own]
+            totals = [pltpu.roll(t, 126, 1) + pltpu.roll(t, 125, 1) for t in tiles] + [total_own]
+            top = functools.reduce(jnp.maximum, tops)
+            factors = [jnp.exp2(t - top) for t in tops]
+            whole = functools.reduce(jnp.add, [f * t for f, t in zip(factors, totals)])
+            factors = [f / whole for f in factors]
+            for i, at in enumerate(mine):
+                parts = [b[i].astype(f32) for b in blocks] + [so[at : at + 8, :]]
+                out = functools.reduce(
+                    jnp.add, [p * f[:, 16 * i : 16 * i + 1] for p, f in zip(parts, factors)]
+                )
+                so[at : at + 8, :] = out
+
+    def final_row(o):
+        j, g, r = o // 32, (o // 2) % 16, o % 2
+        return (g // 8 + c) % 2 * 64 + g % 8 * 8 + j * 2 + r
+
+    out_ref[...] = dot(one_hot((128, 128), final_row), so[...].astype(bf16)).astype(bf16)
     for copy in started:
         copy.wait_send()
 
 
-COPIES = 15 + 7 * CHUNKS + 3 * CHUNKS * 2 + 7 + 2
+COPIES = 15 + 7 + 7 * CHUNKS + 3 * (CHUNKS // 2) + 7 * (CHUNKS - CHUNKS // 2) + 3 * CHUNKS + 15 * CHUNKS
 
 
 def body(queries, prefix_keys, prefix_values, suffix_keys, suffix_values, lengths):
@@ -298,7 +329,7 @@
     out = pl.pallas_call(
         kernel,
         name="attend",
-        out_shape=jax.ShapeDtypeStruct((4, 2, 16, 128), bf16),
+        out_shape=jax.ShapeDtypeStruct((128, 128), bf16),
         in_specs=[pl.BlockSpec(memory_space=pltpu.SMEM)] + [anyspace] * 5,
         out_specs=pl.BlockSpec(memory_space=vmem),
         scratch_shapes=[
@@ -313,23 +344,18 @@
             vmem((128, 128), bf16),
             vmem((4, HEADS, TALL, 128), bf16),
             vmem((4, HEADS, TALL, 128), bf16),
-            vmem((TALL, 1024), bf16),
-            vmem((1024, 1024), bf16),
-            vmem((8, TALL, 128), bf16),
-            vmem((8, TALL, 128), bf16),
+            vmem((CHUNKS, 128, 128), bf16),
+            vmem((CHUNKS, 16, PER + 1, 8, 128), bf16),
+            vmem((CHUNKS, 16, PER + 1, 8, 128), bf16),
             vmem((128, 128), f32),
             vmem((128, 128), f32),
             vmem((128, 128), f32),
-            vmem((TALL, 128), bf16),
-            vmem((TALL, 128), bf16),
-            vmem((4, 16, 128), bf16),
-            vmem((4, 16, 128), bf16),
             pltpu.SemaphoreType.DMA((5,)),
             pltpu.SemaphoreType.DMA((COPIES,)),
             pltpu.SemaphoreType.DMA((COPIES,)),
         ],
         compiler_params=pltpu.CompilerParams(
-            collective_id=0, has_side_effects=True, vmem_limit_bytes=48 * 2**20
+            collective_id=0, has_side_effects=True, vmem_limit_bytes=67_043_328
         ),
     )(
         lengths,

time: 62.4 us -> 49.8 us (0.80)
  Pallas kernels: 56 us -> 47.6 us
  local copies, waits for them, and re-layouts: 5.45 us -> 1.38 us
    pallas_call x1, Pallas kernels: 56 us -> 47.6 us  [body(): pl.pallas_call(kernel, name='attend', out_shape=jax.ShapeDtypeStruct((128...]
    unnamed x9 -> x1, local copies, waits for them, and re-layouts: 5.45 us -> 1.38 us
where the time goes in v2:
time: 49.8 us; the launch traced here: 49.6 us
  Pallas kernels  47.6 us (96%)
  local copies, waits for them, and re-layouts  1.38 us (3%)
  between operations  0.66 us (1%)
    pallas_call x1, Pallas kernels, body(): pl.pallas_call(kernel, name='attend', out_shape=jax.ShapeDtypeStruct((128...  47.6 us
    unnamed x1, local copies, waits for them, and re-layouts  1.38 us

profile of v2, /device:TPU:1, one launch (start us, length us, event | category | flops | bytes accessed | tf_op | source)
XLA Modules:
  0.0 49.6 jit_solution(2033026920309015763)
XLA Ops:
  0.7 47.6 %attend.1 = bf16[128,128]{1,0:T(8,128)(2,1)} custom-call(s32[1]{0:T(128)S(6)} %copy.8.len_ref, bf16[128,128]{1,0:T(8,128)(2,1)} %bitcast.11, bf16[1024,128]{1,0:T(8,128)(2,1)} %bitcast.8, bf16[1024,128]{1,0:T(8,128)(2,1)} %bitcast.9, bf16[16384,128]{1,0:T(8,128)(2,1)} %bitcast.6, bf16[16384,128]{1,0:T(8,128)(2,1)} %bitcast.7), custom_call_target="tpu_custom_call" | custom-call | tf_op jit(solution)/shard_map/attend/pallas_call | solution.py:329
  48.3 1.4 %copy.9 = bf16[1,4,32,128]{3,2,1,0:T(8,128)(2,1)} copy(bf16[1,4,32,128]{3,2,1,0:T(8,128)(2,1)} %bitcast.10) | data formatting | bytes 65536

commit v3 on v2

--- a/solution.py
+++ b/solution.py
@@ -13,8 +13,20 @@
 HIDDEN = -1e30
 
 HEADS = 8
-CHUNKS = 4
-PER = HEADS // CHUNKS
+SIZES = (1, 1, 2, 2, 1, 1)
+STARTS = tuple(sum(SIZES[:k]) for k in range(len(SIZES)))
+CHUNKS = len(SIZES)
+EARLY = 3
+LAST = (3, 3, 3, 3, 5, 5)
+TAILS = tuple(sorted(set(LAST)))
+
+
+def tile_of(head):
+    return head + sum(STARTS[t] + SIZES[t] <= head for t in TAILS)
+
+
+TILES = HEADS + len(TAILS)
+SEMS = 3 + 4 * CHUNKS
 TALL = 144
 PIECE = 2048
 
@@ -85,13 +97,6 @@
     so, sm, sl, local_sem, send_sem, recv_sem,
 ):
     x, y, z, c = place()
-    peers = [dict(dx=d, e=e) for d in (1, 3) for e in (0, 1)] + [dict(e=1)]
-    peers += [dict(dy=d, e=e) for d in (1, 2, 3) for e in (0, 1)]
-    peers += [dict(dz=d, e=e) for d in range(1, 8) for e in (0, 1)]
-    barrier = pltpu.get_barrier_semaphore()
-    for p in peers:
-        pl.semaphore_signal(barrier, inc=1, device_id=device(**p), device_id_type=MESH)
-
     loads = [
         pltpu.make_async_copy(src, dst, local_sem.at[i])
         for i, (src, dst) in enumerate(
@@ -101,20 +106,34 @@
     for load in loads:
         load.start()
 
-    started = []
-
-    def send(src, dst, **to):
-        i = len(started)
-        copy = pltpu.make_async_remote_copy(
-            src_ref=src, dst_ref=dst, send_sem=send_sem.at[i], recv_sem=recv_sem.at[i],
+    peers = [dict(dx=d, e=e) for d in (1, 3) for e in (0, 1)] + [dict(e=1)]
+    peers += [dict(dy=d, e=e) for d in (1, 2, 3) for e in (0, 1)]
+    peers += [dict(dz=d, e=e) for d in range(1, 8) for e in (0, 1)]
+    barrier = pltpu.get_barrier_semaphore()
+    for p in peers:
+        pl.semaphore_signal(barrier, inc=1, device_id=device(**p), device_id_type=MESH)
+
+    groups = []
+
+    def send(group, src, dst, sem=None, **to):
+        pltpu.make_async_remote_copy(
+            src_ref=src, dst_ref=dst, send_sem=send_sem.at[group],
+            recv_sem=recv_sem.at[group if sem is None else sem],
             device_id=device(**to), device_id_type=MESH,
-        )
-        copy.start()
-        started.append(copy)
-        return copy
-
-    def heads_of(k, n=1):
-        return pl.ds(k * PER, n * PER)
+        ).start()
+
+    def new_group(arrivals):
+        groups.append(arrivals)
+        return len(groups) - 1
+
+    def wait_for(sem, ref):
+        pltpu.make_async_copy(ref, ref, sem).wait()
+
+    def arrived(group):
+        wait_for(recv_sem.at[group], groups[group])
+
+    def heads_of(k, last=None):
+        return pl.ds(STARTS[k], sum(SIZES[k : (k if last is None else last) + 1]))
 
     def head_row(o):
         big = o // 16
@@ -141,36 +160,46 @@
 
     pl.semaphore_wait(barrier, len(peers))
 
-    kv_copies = [dict() for _ in range(CHUNKS)]
+    kv_groups = [new_group(kv.at[:, heads_of(k), 1:8]) for k in range(CHUNKS)]
 
     def send_kv(k):
         h = heads_of(k)
         for dx, e in ((1, 0), (3, 1), (1, 1), (3, 0), (0, 1)):
             src = kvs.at[:, h] if e else kv.at[:, h, 0]
-            kv_copies[k][dx, e] = send(src, kv.at[:, h, 2 * dx + e], dx=dx, e=e)
+            relayed = {(1, 0): SEMS + k, (3, 1): SEMS + CHUNKS + k}.get((dx, e))
+            send(kv_groups[k], src, kv.at[:, h, 2 * dx + e], sem=relayed, dx=dx, e=e)
 
     def forward_kv(k):
         h = heads_of(k)
-        kv_copies[k][1, 0].wait_recv()
-        kv_copies[k][2, 0] = send(kv.at[:, h, 2], kv.at[:, h, 4], dx=1)
-        kv_copies[k][3, 1].wait_recv()
-        kv_copies[k][2, 1] = send(kv.at[:, h, 7], kv.at[:, h, 5], dx=3)
-
-    half = CHUNKS // 2
-    zy, yz = heads_of(0, half), heads_of(half, half)
+        wait_for(recv_sem.at[SEMS + k], kv.at[:, h, 2])
+        send(kv_groups[k], kv.at[:, h, 2], kv.at[:, h, 4], dx=1)
+        wait_for(recv_sem.at[SEMS + CHUNKS + k], kv.at[:, h, 7])
+        send(kv_groups[k], kv.at[:, h, 7], kv.at[:, h, 5], dx=3)
+
+    def kv_arrived(k):
+        wait_for(recv_sem.at[kv_groups[k]], kv.at[:, heads_of(k), 1:6])
+
+    zy, yz = heads_of(1, EARLY - 1), heads_of(EARLY, CHUNKS - 1)
 
     def source(e, h):
         return qs.at[h] if e else qy.at[0, 0, 0, h]
 
+    def send_q1(h, n):
+        group = new_group(r2.at[1:16, 0:n])
+        for dz in (4, 3, 5, 2, 6, 1, 7, 0):
+            for e in (0, 1):
+                if dz or e:
+                    send(group, source(e, h), qy.at[0, dz, e, h], dz=dz, e=e)
+        return group
+
     send_kv(0)
-    q1 = [
-        send(source(e, zy), qy.at[0, dz, e, zy], dz=dz, e=e)
-        for dz in (4, 3, 5, 2, 6, 1, 7, 0) for e in (0, 1) if dz or e
-    ]
-    p1 = [
-        send(source(e, yz), qy.at[dy, 0, e, yz], dy=dy, e=e)
-        for dy in (2, 1, 3, 0) for e in (0, 1) if dy or e
-    ]
+    q1a = send_q1(heads_of(0), SIZES[0])
+    p1 = new_group(r2.at[1:8, 0 : HEADS - STARTS[EARLY]])
+    for dy in (2, 1, 3, 0):
+        for e in (0, 1):
+            if dy or e:
+                send(p1, source(e, yz), qy.at[dy, 0, e, yz], dy=dy, e=e)
+    q1b = send_q1(zy, STARTS[EARLY] - STARTS[1])
     send_kv(1)
 
     so[...] = jnp.zeros_like(so)
@@ -205,34 +234,40 @@
     def suffix(first, last):
         lax.fori_loop(first, last, suffix_piece, 0)
 
-    suffix(0, 2)
-    for copy in p1:
-        copy.wait_recv()
-    q2 = [[] for _ in range(CHUNKS)]
+    q2 = {}
 
     def send_q_z(k):
         h = heads_of(k)
-        q2[k] = [send(qy.at[:, 0, :, h], qy.at[:, dz, :, h], dz=dz) for dz in (4, 3, 5, 2, 6, 1, 7)]
+        q2[k] = new_group(qy.at[:, 1:8, :, h])
+        for dz in (4, 3, 5, 2, 6, 1, 7):
+            send(q2[k], qy.at[:, 0, :, h], qy.at[:, dz, :, h], dz=dz)
 
     def send_q_y(k):
         h = heads_of(k)
-        q2[k] = [send(qy.at[0, :, :, h], qy.at[dy, :, :, h], dy=dy) for dy in (2, 1, 3)]
-
-    for k in range(half, CHUNKS):
+        q2[k] = new_group(qy.at[1:4, :, :, h])
+        for dy in (2, 1, 3):
+            send(q2[k], qy.at[0, :, :, h], qy.at[dy, :, :, h], dy=dy)
+
+    suffix(0, 2)
+    forward_kv(0)
+    send_kv(2)
+    arrived(p1)
+    for k in range(EARLY, CHUNKS):
         send_q_z(k)
     suffix(2, 3)
-    forward_kv(0)
-    send_kv(2)
-    suffix(3, 5)
-    for copy in q1:
-        copy.wait_recv()
-    for k in range(half):
-        send_q_y(k)
-    suffix(5, 6)
+    arrived(q1a)
+    send_q_y(0)
     forward_kv(1)
     send_kv(3)
+    suffix(3, 4)
+    arrived(q1b)
+    for k in range(1, EARLY):
+        send_q_y(k)
+    suffix(4, 6)
+    forward_kv(2)
+    send_kv(4)
+    send_kv(5)
     suffix(6, 16384 // PIECE)
-    forward_kv(2)
 
     eye = one_hot((128, 128), lambda o: o)
 
@@ -254,78 +289,90 @@
     rs2 = []
 
     def over_y(k):
-        for copy in rs1[k]:
-            copy.wait_recv()
-        for i in range(PER):
-            g = k * PER + i
+        arrived(rs1[k])
+        first, n = tile_of(STARTS[k]), SIZES[k]
+        for i in range(n):
+            g = STARTS[k] + i
             out, top, total = merged([xs[0, g]] + [r1[dy, g] for dy in range(1, 4)])
             mh, ml = in_two(top)
             adjust = jnp.exp2(top - (mh + ml))
-            ys[k, :, i] = dot_t(eye, (out * adjust).astype(bf16)).astype(bf16).reshape(16, 8, 128)
-            sx[k, 16 * i : 16 * i + 16, :] = packed_stats(mh, ml, total * adjust)
-        ys[k, :, PER] = dot_t(eye, sx[k]).astype(bf16).reshape(16, 8, 128)
-        rs2.append(
-            [
-                send(ys.at[k, 2 * dz + e], r2.at[k, 2 * dz + e], dz=8 - dz, e=e)
-                for dz in (4, 3, 5, 2, 6, 1, 7, 0) for e in (0, 1) if dz or e
-            ]
-        )
-
-    for k in range(CHUNKS):
-        for copy in q2[k]:
-            copy.wait_recv()
-        for at in ((0, 1), (1, 1), (3, 0), (2, 0), (2, 1)):
-            kv_copies[k][at].wait_recv()
-        lax.fori_loop(k * PER, (k + 1) * PER, prompt_head, 0)
+            ys[:, first + i] = dot_t(eye, (out * adjust).astype(bf16)).astype(bf16).reshape(16, 8, 128)
+            sx[TAILS.index(LAST[k]), 16 * g : 16 * g + 16, :] = packed_stats(mh, ml, total * adjust)
+        if k in TAILS:
+            stats = dot_t(eye, sx[TAILS.index(k)]).astype(bf16)
+            ys[:, first + n] = stats.reshape(16, 8, 128)
+            n += 1
+        t = pl.ds(first, n)
+        rs2.append(new_group(r2.at[1:16, t]))
+        for dz in (4, 3, 5, 2, 6, 1, 7, 0):
+            for e in (0, 1):
+                if dz or e:
+                    send(rs2[k], ys.at[2 * dz + e, t], r2.at[2 * dz + e, t], dz=8 - dz, e=e)
+
+    def prompt(k):
+        arrived(q2[k])
+        kv_arrived(k)
+        lax.fori_loop(STARTS[k], STARTS[k] + SIZES[k], prompt_head, 0)
         h = heads_of(k)
-        rs1.append([send(xs.at[dy, h], r1.at[dy, h], dy=4 - dy) for dy in (2, 1, 3)])
-        if k == 0:
-            forward_kv(3)
-        if k >= 2:
-            over_y(k - 2)
-    for k in range(CHUNKS - 2, CHUNKS):
+        rs1.append(new_group(r1.at[1:4, h]))
+        for dy in (2, 1, 3):
+            send(rs1[k], xs.at[dy, h], r1.at[dy, h], dy=4 - dy)
+
+    prompt(0)
+    prompt(1)
+    forward_kv(3)
+    forward_kv(4)
+    prompt(2)
+    forward_kv(5)
+    over_y(0)
+    over_y(1)
+    prompt(3)
+    prompt(4)
+    prompt(5)
+    for k in range(2, CHUNKS):
         over_y(k)
 
-    done = []
-    for k in range(CHUNKS):
-        for copy in rs2[k]:
-            copy.wait_recv()
+    begun = 0
+    for tail in TAILS:
+        mine = range(begun, tail + 1)
+        begun = tail + 1
+        for k in mine:
+            arrived(rs2[k])
+        heads = range(STARTS[mine[0]], STARTS[tail] + SIZES[tail])
+        at_stats = tile_of(heads[-1]) + 1
         for e in (0, 1):
-            blocks = [ys.at[k, 0] if not (dz or e) else r2.at[k, 2 * dz + e] for dz in range(8)]
+            blocks = [r2.at[2 * dz + e] if dz or e else ys.at[0] for dz in range(8)]
             lane = iota((8, 128), 1)
-            mine = [(e * 8 + k * PER + i) * 8 for i in range(PER)]
             top_own = total_own = jnp.zeros((8, 128), f32)
-            for i, at in enumerate(mine):
-                top_own = jnp.where(lane // 16 == i, sm[at : at + 8, :], top_own)
-                total_own = jnp.where(lane // 16 == i, sl[at : at + 8, :], total_own)
-            tiles = [b[PER].astype(f32) for b in blocks]
+            for g in heads:
+                at = (e * 8 + g) * 8
+                top_own = jnp.where(lane // 16 == g, sm[at : at + 8, :], top_own)
+                total_own = jnp.where(lane // 16 == g, sl[at : at + 8, :], total_own)
+            tiles = [b[at_stats].astype(f32) for b in blocks]
             tops = [t + pltpu.roll(t, 127, 1) for t in tiles] + [top_own]
             totals = [pltpu.roll(t, 126, 1) + pltpu.roll(t, 125, 1) for t in tiles] + [total_own]
             top = functools.reduce(jnp.maximum, tops)
             factors = [jnp.exp2(t - top) for t in tops]
             whole = functools.reduce(jnp.add, [f * t for f, t in zip(factors, totals)])
             factors = [f / whole for f in factors]
-            for i, at in enumerate(mine):
-                parts = [b[i].astype(f32) for b in blocks] + [so[at : at + 8, :]]
-                out = functools.reduce(
-                    jnp.add, [p * f[:, 16 * i : 16 * i + 1] for p, f in zip(parts, factors)]
+            for g in heads:
+                at = (e * 8 + g) * 8
+                parts = [b[tile_of(g)].astype(f32) for b in blocks] + [so[at : at + 8, :]]
+                so[at : at + 8, :] = functools.reduce(
+                    jnp.add, [p * f[:, 16 * g : 16 * g + 1] for p, f in zip(parts, factors)]
                 )
-                so[at : at + 8, :] = out
 
     def final_row(o):
         j, g, r = o // 32, (o // 2) % 16, o % 2
         return (g // 8 + c) % 2 * 64 + g % 8 * 8 + j * 2 + r
 
     out_ref[...] = dot(one_hot((128, 128), final_row), so[...].astype(bf16)).astype(bf16)
-    for copy in started:
-        copy.wait_send()
-
-
-COPIES = 15 + 7 + 7 * CHUNKS + 3 * (CHUNKS // 2) + 7 * (CHUNKS - CHUNKS // 2) + 3 * CHUNKS + 15 * CHUNKS
+    for group, arrivals in enumerate(groups):
+        wait_for(send_sem.at[group], arrivals)
 
 
 def body(queries, prefix_keys, prefix_values, suffix_keys, suffix_values, lengths):
-    vmem, anyspace = pltpu.VMEM, pl.BlockSpec(memory_space=pl.ANY)
+    vmem, anyspace = pltpu.VMEM, pl.BlockSpec(memory_space=pltpu.HBM)
     out = pl.pallas_call(
         kernel,
         name="attend",
@@ -344,15 +391,15 @@
             vmem((128, 128), bf16),
             vmem((4, HEADS, TALL, 128), bf16),
             vmem((4, HEADS, TALL, 128), bf16),
-            vmem((CHUNKS, 128, 128), bf16),
-            vmem((CHUNKS, 16, PER + 1, 8, 128), bf16),
-            vmem((CHUNKS, 16, PER + 1, 8, 128), bf16),
+            vmem((len(TAILS), 128, 128), bf16),
+            vmem((16, TILES, 8, 128), bf16),
+            vmem((16, TILES, 8, 128), bf16),
             vmem((128, 128), f32),
             vmem((128, 128), f32),
             vmem((128, 128), f32),
             pltpu.SemaphoreType.DMA((5,)),
-            pltpu.SemaphoreType.DMA((COPIES,)),
-            pltpu.SemaphoreType.DMA((COPIES,)),
+            pltpu.SemaphoreType.DMA((SEMS,)),
+            pltpu.SemaphoreType.DMA((SEMS + 2 * CHUNKS,)),
         ],
         compiler_params=pltpu.CompilerParams(
             collective_id=0, has_side_effects=True, vmem_limit_bytes=67_043_328

time: 49.8 us -> 46.7 us (0.938)
  Pallas kernels: 47.6 us -> 44.5 us
    pallas_call x1, Pallas kernels: 47.6 us -> 44.5 us  [body(): pl.pallas_call(kernel, name='attend', out_shape=jax.ShapeDtypeStruct((128...]
where the time goes in v3:
time: 46.7 us; the launch traced here: 46.6 us
  Pallas kernels  44.5 us (95%)
  local copies, waits for them, and re-layouts  1.38 us (3%)
  between operations  0.66 us (1%)
    pallas_call x1, Pallas kernels, body(): pl.pallas_call(kernel, name='attend', out_shape=jax.ShapeDtypeStruct((128...  44.5 us
    unnamed x1, local copies, waits for them, and re-layouts  1.38 us

profile of v3, /device:TPU:1, one launch (start us, length us, event | category | flops | bytes accessed | tf_op | source)
XLA Modules:
  0.0 46.6 jit_solution(10640830191513244635)
XLA Ops:
  0.7 44.5 %attend.1 = bf16[128,128]{1,0:T(8,128)(2,1)} custom-call(s32[1]{0:T(128)S(6)} %copy.8.len_ref, bf16[128,128]{1,0:T(8,128)(2,1)} %bitcast.11, bf16[1024,128]{1,0:T(8,128)(2,1)} %bitcast.8, bf16[1024,128]{1,0:T(8,128)(2,1)} %bitcast.9, bf16[16384,128]{1,0:T(8,128)(2,1)} %bitcast.6, bf16[16384,128]{1,0:T(8,128)(2,1)} %bitcast.7), custom_call_target="tpu_custom_call" | custom-call | tf_op jit(solution)/shard_map/attend/pallas_call | solution.py:376
  45.2 1.4 %copy.9 = bf16[1,4,32,128]{3,2,1,0:T(8,128)(2,1)} copy(bf16[1,4,32,128]{3,2,1,0:T(8,128)(2,1)} %bitcast.10) | data formatting | bytes 65536

commit v4 on v3

--- a/solution.py
+++ b/solution.py
@@ -13,11 +13,11 @@
 HIDDEN = -1e30
 
 HEADS = 8
-SIZES = (1, 1, 2, 2, 1, 1)
+SIZES = (1,) * HEADS
 STARTS = tuple(sum(SIZES[:k]) for k in range(len(SIZES)))
 CHUNKS = len(SIZES)
-EARLY = 3
-LAST = (3, 3, 3, 3, 5, 5)
+EARLY = 4
+LAST = (3,) * 4 + (7,) * 4
 TAILS = tuple(sorted(set(LAST)))
 
 
@@ -27,7 +27,7 @@
 
 TILES = HEADS + len(TAILS)
 SEMS = 3 + 4 * CHUNKS
-TALL = 144
+TALL = 136
 PIECE = 2048
 
 f32, bf16 = jnp.float32, jnp.bfloat16
@@ -70,7 +70,7 @@
 
 def packed_stats(mh, ml, total):
     lh, ll = in_two(total)
-    row = iota((16, mh.shape[1]), 0)
+    row = iota((8, mh.shape[1]), 0)
     out = jnp.where(row == 0, mh, jnp.where(row == 1, ml, jnp.where(row == 2, lh, ll)))
     return jnp.where(row < 4, out, 0.0).astype(bf16)
 
@@ -201,6 +201,7 @@
                 send(p1, source(e, yz), qy.at[dy, 0, e, yz], dy=dy, e=e)
     q1b = send_q1(zy, STARTS[EARLY] - STARTS[1])
     send_kv(1)
+    send_kv(2)
 
     so[...] = jnp.zeros_like(so)
     sl[...] = jnp.zeros_like(sl)
@@ -248,26 +249,26 @@
         for dy in (2, 1, 3):
             send(q2[k], qy.at[0, :, :, h], qy.at[dy, :, :, h], dy=dy)
 
-    suffix(0, 2)
-    forward_kv(0)
-    send_kv(2)
+    suffix(0, 3)
     arrived(p1)
     for k in range(EARLY, CHUNKS):
         send_q_z(k)
-    suffix(2, 3)
+    forward_kv(0)
+    send_kv(3)
     arrived(q1a)
     send_q_y(0)
+    suffix(3, 4)
     forward_kv(1)
-    send_kv(3)
-    suffix(3, 4)
+    send_kv(4)
     arrived(q1b)
     for k in range(1, EARLY):
         send_q_y(k)
     suffix(4, 6)
     forward_kv(2)
-    send_kv(4)
     send_kv(5)
     suffix(6, 16384 // PIECE)
+    forward_kv(3)
+    send_kv(6)
 
     eye = one_hot((128, 128), lambda o: o)
 
@@ -297,7 +298,7 @@
             mh, ml = in_two(top)
             adjust = jnp.exp2(top - (mh + ml))
             ys[:, first + i] = dot_t(eye, (out * adjust).astype(bf16)).astype(bf16).reshape(16, 8, 128)
-            sx[TAILS.index(LAST[k]), 16 * g : 16 * g + 16, :] = packed_stats(mh, ml, total * adjust)
+            sx[TAILS.index(LAST[k]), 16 * g : 16 * g + 8, :] = packed_stats(mh, ml, total * adjust)
         if k in TAILS:
             stats = dot_t(eye, sx[TAILS.index(k)]).astype(bf16)
             ys[:, first + n] = stats.reshape(16, 8, 128)
@@ -319,17 +320,23 @@
             send(rs1[k], xs.at[dy, h], r1.at[dy, h], dy=4 - dy)
 
     prompt(0)
+    forward_kv(4)
+    send_kv(7)
     prompt(1)
-    forward_kv(3)
-    forward_kv(4)
     prompt(2)
     forward_kv(5)
+    prompt(3)
     over_y(0)
+    forward_kv(6)
+    prompt(4)
     over_y(1)
-    prompt(3)
-    prompt(4)
+    forward_kv(7)
     prompt(5)
-    for k in range(2, CHUNKS):
+    over_y(2)
+    prompt(6)
+    over_y(3)
+    prompt(7)
+    for k in range(4, CHUNKS):
         over_y(k)
 
     begun = 0

time: 46.7 us -> 44.9 us (0.961)
  Pallas kernels: 44.5 us -> 42.7 us
    pallas_call x1, Pallas kernels: 44.5 us -> 42.7 us  [body(): pl.pallas_call(kernel, name='attend', out_shape=jax.ShapeDtypeStruct((128...]
where the time goes in v4:
time: 44.9 us; the launch traced here: 44.8 us
  Pallas kernels  42.7 us (95%)
  local copies, waits for them, and re-layouts  1.38 us (3%)
  between operations  0.66 us (1%)
    pallas_call x1, Pallas kernels, body(): pl.pallas_call(kernel, name='attend', out_shape=jax.ShapeDtypeStruct((128...  42.7 us
    unnamed x1, local copies, waits for them, and re-layouts  1.38 us

profile of v4, /device:TPU:1, one launch (start us, length us, event | category | flops | bytes accessed | tf_op | source)
XLA Modules:
  0.0 44.8 jit_solution(409809525722049567)
XLA Ops:
  0.7 42.7 %attend.1 = bf16[128,128]{1,0:T(8,128)(2,1)} custom-call(s32[1]{0:T(128)S(6)} %copy.8.len_ref, bf16[128,128]{1,0:T(8,128)(2,1)} %bitcast.11, bf16[1024,128]{1,0:T(8,128)(2,1)} %bitcast.8, bf16[1024,128]{1,0:T(8,128)(2,1)} %bitcast.9, bf16[16384,128]{1,0:T(8,128)(2,1)} %bitcast.6, bf16[16384,128]{1,0:T(8,128)(2,1)} %bitcast.7), custom_call_target="tpu_custom_call" | custom-call | tf_op jit(solution)/shard_map/attend/pallas_call | solution.py:383
  43.4 1.4 %copy.9 = bf16[1,4,32,128]{3,2,1,0:T(8,128)(2,1)} copy(bf16[1,4,32,128]{3,2,1,0:T(8,128)(2,1)} %bitcast.10) | data formatting | bytes 65536

commit v5 on v4

--- a/solution.py
+++ b/solution.py
@@ -92,15 +92,15 @@
 
 
 def kernel(
-    len_ref, q_hbm, k_hbm, v_hbm, sk_hbm, sv_hbm, out_ref,
+    len_hbm, q_hbm, k_hbm, v_hbm, sk_hbm, sv_hbm, out_ref,
     qin, kvin, sk, sv, kv, kvs, qy, qs, qsuf, xs, r1, sx, ys, r2,
-    so, sm, sl, local_sem, send_sem, recv_sem,
+    so, sm, sl, len_ref, local_sem, send_sem, recv_sem,
 ):
     x, y, z, c = place()
     loads = [
         pltpu.make_async_copy(src, dst, local_sem.at[i])
         for i, (src, dst) in enumerate(
-            [(k_hbm, kvin.at[0]), (v_hbm, kvin.at[1]), (q_hbm, qin), (sk_hbm, sk), (sv_hbm, sv)]
+            [(k_hbm, kvin.at[0]), (v_hbm, kvin.at[1]), (q_hbm, qin), (len_hbm, len_ref), (sk_hbm, sk), (sv_hbm, sv)]
         )
     ]
     for load in loads:
@@ -117,7 +117,7 @@
 
     def send(group, src, dst, sem=None, **to):
         pltpu.make_async_remote_copy(
-            src_ref=src, dst_ref=dst, send_sem=send_sem.at[group],
+            src_ref=src, dst_ref=dst, send_sem=send_sem,
             recv_sem=recv_sem.at[group if sem is None else sem],
             device_id=device(**to), device_id_type=MESH,
         ).start()
@@ -147,17 +147,6 @@
             kv[t, :, 0, 16 * b : 16 * b + 16, :] = m[:8]
             kvs[t, :, 16 * b : 16 * b + 16, :] = m[8:]
 
-    loads[2].wait()
-
-    def query_row(o):
-        e, g, j, r = o // 64, (o // 8) % 8, (o % 8) // 2, o % 2
-        return j * 32 + ((e + c) % 2 * 8 + g) * 2 + r
-
-    q = dot(one_hot((128, 128), query_row), qin[...]).astype(bf16)
-    qsuf[...] = q
-    qy[0, 0, 0] = q[:64].reshape(HEADS, 8, 128)
-    qs[...] = q[64:].reshape(HEADS, 8, 128)
-
     pl.semaphore_wait(barrier, len(peers))
 
     kv_groups = [new_group(kv.at[:, heads_of(k), 1:8]) for k in range(CHUNKS)]
@@ -166,14 +155,13 @@
         h = heads_of(k)
         for dx, e in ((1, 0), (3, 1), (1, 1), (3, 0), (0, 1)):
             src = kvs.at[:, h] if e else kv.at[:, h, 0]
-            relayed = {(1, 0): SEMS + k, (3, 1): SEMS + CHUNKS + k}.get((dx, e))
+            relayed = SEMS + k if (dx, e) in ((1, 0), (3, 1)) else None
             send(kv_groups[k], src, kv.at[:, h, 2 * dx + e], sem=relayed, dx=dx, e=e)
 
     def forward_kv(k):
         h = heads_of(k)
-        wait_for(recv_sem.at[SEMS + k], kv.at[:, h, 2])
+        wait_for(recv_sem.at[SEMS + k], kv.at[:, h, 2:4])
         send(kv_groups[k], kv.at[:, h, 2], kv.at[:, h, 4], dx=1)
-        wait_for(recv_sem.at[SEMS + CHUNKS + k], kv.at[:, h, 7])
         send(kv_groups[k], kv.at[:, h, 7], kv.at[:, h, 5], dx=3)
 
     def kv_arrived(k):
@@ -193,6 +181,17 @@
         return group
 
     send_kv(0)
+    loads[2].wait()
+
+    def query_row(o):
+        e, g, j, r = o // 64, (o // 8) % 8, (o % 8) // 2, o % 2
+        return j * 32 + ((e + c) % 2 * 8 + g) * 2 + r
+
+    q = dot(one_hot((128, 128), query_row), qin[...]).astype(bf16)
+    qsuf[...] = q
+    qy[0, 0, 0] = q[:64].reshape(HEADS, 8, 128)
+    qs[...] = q[64:].reshape(HEADS, 8, 128)
+
     q1a = send_q1(heads_of(0), SIZES[0])
     p1 = new_group(r2.at[1:8, 0 : HEADS - STARTS[EARLY]])
     for dy in (2, 1, 3, 0):
@@ -207,8 +206,8 @@
     sl[...] = jnp.zeros_like(sl)
     sm[...] = jnp.full_like(sm, HIDDEN)
     sx[...] = jnp.zeros_like(sx)
-    loads[3].wait()
-    loads[4].wait()
+    for load in loads[3:]:
+        load.wait()
     length = len_ref[0]
 
     def suffix_piece(i, _):
@@ -250,23 +249,22 @@
             send(q2[k], qy.at[0, :, :, h], qy.at[dy, :, :, h], dy=dy)
 
     suffix(0, 3)
+    forward_kv(0)
+    send_kv(3)
     arrived(p1)
     for k in range(EARLY, CHUNKS):
         send_q_z(k)
-    forward_kv(0)
-    send_kv(3)
     arrived(q1a)
     send_q_y(0)
-    suffix(3, 4)
     forward_kv(1)
     send_kv(4)
     arrived(q1b)
     for k in range(1, EARLY):
         send_q_y(k)
-    suffix(4, 6)
+    suffix(3, 4)
     forward_kv(2)
     send_kv(5)
-    suffix(6, 16384 // PIECE)
+    suffix(4, 5)
     forward_kv(3)
     send_kv(6)
 
@@ -338,6 +336,7 @@
     prompt(7)
     for k in range(4, CHUNKS):
         over_y(k)
+    suffix(5, 16384 // PIECE)
 
     begun = 0
     for tail in TAILS:
@@ -374,8 +373,8 @@
         return (g // 8 + c) % 2 * 64 + g % 8 * 8 + j * 2 + r
 
     out_ref[...] = dot(one_hot((128, 128), final_row), so[...].astype(bf16)).astype(bf16)
-    for group, arrivals in enumerate(groups):
-        wait_for(send_sem.at[group], arrivals)
+    sent = sum(math.prod(arrivals.shape) for arrivals in groups)
+    wait_for(send_sem, sk.at[0 : sent // 128])
 
 
 def body(queries, prefix_keys, prefix_values, suffix_keys, suffix_values, lengths):
@@ -384,7 +383,7 @@
         kernel,
         name="attend",
         out_shape=jax.ShapeDtypeStruct((128, 128), bf16),
-        in_specs=[pl.BlockSpec(memory_space=pltpu.SMEM)] + [anyspace] * 5,
+        in_specs=[anyspace] * 6,
         out_specs=pl.BlockSpec(memory_space=vmem),
         scratch_shapes=[
             vmem((128, 128), bf16),
@@ -404,9 +403,10 @@
             vmem((128, 128), f32),
             vmem((128, 128), f32),
             vmem((128, 128), f32),
-            pltpu.SemaphoreType.DMA((5,)),
-            pltpu.SemaphoreType.DMA((SEMS,)),
-            pltpu.SemaphoreType.DMA((SEMS + 2 * CHUNKS,)),
+            pltpu.SMEM((1,), jnp.int32),
+            pltpu.SemaphoreType.DMA((6,)),
+            pltpu.SemaphoreType.DMA,
+            pltpu.SemaphoreType.DMA((SEMS + CHUNKS,)),
         ],
         compiler_params=pltpu.CompilerParams(
             collective_id=0, has_side_effects=True, vmem_limit_bytes=67_043_328

time: 44.9 us -> 44.4 us (0.989)
  Pallas kernels: 42.7 us -> 42.2 us
    pallas_call x1, Pallas kernels: 42.7 us -> 42.2 us  [body(): pl.pallas_call(kernel, name='attend', out_shape=jax.ShapeDtypeStruct((128...]
where the time goes in v5:
time: 44.4 us; the launch traced here: 44.2 us
  Pallas kernels  42.2 us (95%)
  local copies, waits for them, and re-layouts  1.38 us (3%)
  between operations  0.66 us (1%)
    pallas_call x1, Pallas kernels, body(): pl.pallas_call(kernel, name='attend', out_shape=jax.ShapeDtypeStruct((128...  42.2 us
    unnamed x1, local copies, waits for them, and re-layouts  1.38 us

profile of v5, /device:TPU:1, one launch (start us, length us, event | category | flops | bytes accessed | tf_op | source)
XLA Modules:
  0.0 44.2 jit_solution(5848686454231214510)
XLA Ops:
  0.7 42.2 %attend.1 = bf16[128,128]{1,0:T(8,128)(2,1)} custom-call(s32[1]{0:T(128)S(6)} %copy.8.len_hbm, bf16[128,128]{1,0:T(8,128)(2,1)} %bitcast.11, bf16[1024,128]{1,0:T(8,128)(2,1)} %bitcast.8, bf16[1024,128]{1,0:T(8,128)(2,1)} %bitcast.9, bf16[16384,128]{1,0:T(8,128)(2,1)} %bitcast.6, bf16[16384,128]{1,0:T(8,128)(2,1)} %bitcast.7), custom_call_target="tpu_custom_call" | custom-call | tf_op jit(solution)/shard_map/attend/pallas_call | solution.py:382
  42.8 1.4 %copy.9 = bf16[1,4,32,128]{3,2,1,0:T(8,128)(2,1)} copy(bf16[1,4,32,128]{3,2,1,0:T(8,128)(2,1)} %bitcast.10) | data formatting | bytes 65536

commit v6 on v5

--- a/solution.py
+++ b/solution.py
@@ -267,6 +267,7 @@
     suffix(4, 5)
     forward_kv(3)
     send_kv(6)
+    send_kv(7)
 
     eye = one_hot((128, 128), lambda o: o)
 
@@ -319,7 +320,6 @@
 
     prompt(0)
     forward_kv(4)
-    send_kv(7)
     prompt(1)
     prompt(2)
     forward_kv(5)

time: 44.4 us -> 45.1 us (1.016)
  Pallas kernels: 42.2 us -> 42.9 us
    pallas_call x1, Pallas kernels: 42.2 us -> 42.9 us  [body(): pl.pallas_call(kernel, name='attend', out_shape=jax.ShapeDtypeStruct((128...]
where the time goes in v6:
time: 45.1 us; the launch traced here: 44.9 us
  Pallas kernels  42.9 us (95%)
  local copies, waits for them, and re-layouts  1.38 us (3%)
  between operations  0.66 us (1%)
    pallas_call x1, Pallas kernels, body(): pl.pallas_call(kernel, name='attend', out_shape=jax.ShapeDtypeStruct((128...  42.9 us
    unnamed x1, local copies, waits for them, and re-layouts  1.38 us

profile of v6, /device:TPU:1, one launch (start us, length us, event | category | flops | bytes accessed | tf_op | source)
XLA Modules:
  0.0 44.9 jit_solution(16928049775110403995)
XLA Ops:
  0.7 42.9 %attend.1 = bf16[128,128]{1,0:T(8,128)(2,1)} custom-call(s32[1]{0:T(128)S(6)} %copy.8.len_hbm, bf16[128,128]{1,0:T(8,128)(2,1)} %bitcast.11, bf16[1024,128]{1,0:T(8,128)(2,1)} %bitcast.8, bf16[1024,128]{1,0:T(8,128)(2,1)} %bitcast.9, bf16[16384,128]{1,0:T(8,128)(2,1)} %bitcast.6, bf16[16384,128]{1,0:T(8,128)(2,1)} %bitcast.7), custom_call_target="tpu_custom_call" | custom-call | tf_op jit(solution)/shard_map/attend/pallas_call | solution.py:382
  43.6 1.4 %copy.9 = bf16[1,4,32,128]{3,2,1,0:T(8,128)(2,1)} copy(bf16[1,4,32,128]{3,2,1,0:T(8,128)(2,1)} %bitcast.10) | data formatting | bytes 65536
